TPU v7x, 128 devices: a whole 4x4x4 slice. The times are simulated.
128 devices in a mesh: cp: 128 (over x, y, z, core).
Axes of the slice: x: 4, y: 4, z: 4, core: 2. Of those that a mesh axis runs over, the one named last changes fastest.
Arguments:
- raw_inputs: bfloat16 [3584, 229376], P(None, 'cp'), may hold values from -6 to 6
- state_maps: bfloat16 [128, 229376], P(None, 'cp'), may hold values from -6 to 6
- step_size: float32 [56, 229376], P(None, 'cp'), may hold values from 0 to 1, as said below
- log_decay: float32 [56, 229376], P(None, 'cp'), may hold values from -2 to 0, as said below
- conv_weight: float32 [4, 3584], replicated, may hold values from -3 to 3
- conv_bias: float32 [3584], replicated, may hold values from -3 to 3
- skip_gain: float32 [56], replicated, may hold values from 0.5 to 1.5
Outputs:
- layer_output: bfloat16 [3584, 229376], P(None, 'cp')
Inputs may be any that keep to these rules, and one draw needn't show every extreme that they name: step_size is positive. log_decay is never positive.
All inputs are finite; a program needn't handle non-finite values.
Results may differ from a plain program's by a relative error of at most 0.0058.
Values may be sent and summed in bfloat16 or wider, within the bound.
No kernel may reach another device: no remote copies, remote signals or barrier semaphores. Data moves between devices by JAX's collectives and lax.ppermute only.
A program may use at most 192 MiB of HBM per device.

v0:
```python
import functools

import jax
import jax.numpy as jnp
from jax import lax
from jax.experimental import pallas as pl
from jax.experimental.pallas import tpu as pltpu
from jax.sharding import PartitionSpec as P

CHUNK = 128
GROUP = 8
HEAD_DIM = 64
STATE = 64
ROWS = GROUP * HEAD_DIM
LOG2E = 1.4426950408889634
F32 = jnp.float32
BF16 = jnp.bfloat16


def dot_nt(a, b):
    return lax.dot_general(a, b, (((1,), (1,)), ((), ())), preferred_element_type=F32)


def chunk_sums(log_decay, chunks):
    stacked = jnp.concatenate(
        [log_decay[:, c * CHUNK : (c + 1) * CHUNK] for c in range(chunks)], axis=0
    ) * LOG2E
    row = lax.broadcasted_iota(jnp.int32, (CHUNK, CHUNK), 0)
    col = lax.broadcasted_iota(jnp.int32, (CHUNK, CHUNK), 1)
    upper = jnp.where(row <= col, 1.0, 0.0).astype(F32)
    summed = lax.dot_general(
        stacked, upper, (((1,), (0,)), ((), ())),
        precision=lax.Precision.HIGHEST, preferred_element_type=F32,
    )
    return [summed[c * GROUP : (c + 1) * GROUP] for c in range(chunks)]


def values_kernel(chunks, raw_ref, halo_ref, maps_ref, step_ref, decay_ref, taps_ref, bias_ref,
                  x_ref, sums_ref, lead_ref, msg_ref, taps_scr, d_scr, xd_scr, part_scr):
    g = pl.program_id(0)
    half_lanes = 4 * HEAD_DIM
    sums = chunk_sums(decay_ref[...], chunks)
    ends = [jnp.broadcast_to(s[:, CHUNK - 1 :], (GROUP, CHUNK)) for s in sums]
    before = jnp.zeros((GROUP, CHUNK), F32)
    for c in range(chunks):
        at = slice(c * CHUNK, (c + 1) * CHUNK)
        sums_ref[:, at] = sums[c]
        lead_ref[:, at] = jnp.exp2(before + sums[c])
        before = before + ends[c]
    after = jnp.zeros((GROUP, CHUNK), F32)
    for c in reversed(range(chunks)):
        at = slice(c * CHUNK, (c + 1) * CHUNK)
        to_end = jnp.exp2((ends[c] - sums[c]) + after) * step_ref[:, at]
        for h in range(GROUP):
            d_scr[h, :, at] = jnp.broadcast_to(to_end[h : h + 1, :], (8, CHUNK))
        after = after + ends[c]
    total = jnp.exp2(before)

    lane8 = lax.broadcasted_iota(jnp.int32, (GROUP, CHUNK), 1)
    sub8 = lax.broadcasted_iota(jnp.int32, (GROUP, CHUNK), 0)
    own = lane8 == g * 4 + lax.rem(sub8, 4)
    placed = jnp.where(own, total, 0.0)

    @pl.when(g == 0)
    def _():
        part_scr[...] = jnp.zeros_like(part_scr)

    part_scr[...] += placed

    taps = jnp.concatenate([taps_ref[...], bias_ref[...], jnp.zeros((3, ROWS), F32)], axis=0) * 0.5
    taps_scr[...] = jnp.transpose(taps)

    lane = lax.broadcasted_iota(jnp.int32, (16, CHUNK), 1)
    inside = [lane >= k for k in range(4)]
    keys = maps_ref[:STATE, :]

    def pair_body(pair, carry):
        for r in range(8):
            rows = pl.ds(pl.multiple_of(pair * 128 + r * 16, 16), 16)
            local = slice(r * 16, (r + 1) * 16)
            cols = taps_scr[rows, :]
            w = [jnp.broadcast_to(cols[:, k : k + 1], (16, CHUNK)) for k in range(5)]
            head = pair * 2 + r // 4
            last = halo_ref[rows, :].astype(F32)
            prior = [None] + [pltpu.roll(last, k, 1) for k in (1, 2, 3)]
            for c in range(chunks):
                at = slice(c * CHUNK, (c + 1) * CHUNK)
                now = raw_ref[rows, at].astype(F32)
                rolled = [None] + [pltpu.roll(now, k, 1) for k in (1, 2, 3)]
                h = w[4] + w[3] * now
                for k in (1, 2, 3):
                    h = h + w[3 - k] * jnp.where(inside[k], rolled[k], prior[k])
                prior = rolled
                value = h + h * jnp.tanh(h)
                x_ref[rows, at] = value.astype(BF16)
                to_end = d_scr[head, :, at]
                to_end = jnp.concatenate([to_end, to_end], axis=0)
                xd_scr[local, at] = (value * to_end).astype(BF16)
        state = dot_nt(keys, xd_scr[...])
        lanes = pl.ds(pl.multiple_of(g * half_lanes + lax.rem(pair, 2) * 128, 128), 128)
        msg_ref[lax.div(pair, 2), :, lanes] = state.astype(BF16)
        return carry

    lax.fori_loop(0, 4, pair_body, 0)

    @pl.when(g == pl.num_programs(0) - 1)
    def _():
        acc = part_scr[...]
        lane1 = lax.broadcasted_iota(jnp.int32, (1, CHUNK), 1)
        for s in range(2):
            d = acc[4 * s : 4 * s + 1] + acc[4 * s + 1 : 4 * s + 2]
            d = d + (acc[4 * s + 2 : 4 * s + 3] + acc[4 * s + 3 : 4 * s + 4])
            hi = d.astype(BF16).astype(F32)
            mid = (d - hi).astype(BF16).astype(F32)
            low = (d - hi) - mid
            row = hi + pltpu.roll(jnp.broadcast_to(mid, (8, CHUNK)), 32, 1)[:1]
            row = row + pltpu.roll(jnp.broadcast_to(low, (8, CHUNK)), 64, 1)[:1]
            base = msg_ref.shape[2] - CHUNK
            msg_ref[s, :, base:] = jnp.broadcast_to(row, (STATE, CHUNK)).astype(BF16)


def scan_kernel(got_ref, out_ref):
    count = got_ref.shape[0]
    width = out_ref.shape[1]
    row = lax.broadcasted_iota(jnp.int32, (count, 128), 0)
    part = lax.broadcasted_iota(jnp.int32, (128, 128), 0)
    lane = lax.broadcasted_iota(jnp.int32, (128, 128), 1)
    parts = got_ref[:, width:]
    for t in range(width // 128):
        at = slice(t * 128, (t + 1) * 128)
        head = t * 2 + lax.div(lane, 64)
        pick = jnp.where((lax.rem(part, 32) == head) & (part < 96), 1.0, 0.0).astype(BF16)
        decay = jnp.dot(parts, pick, preferred_element_type=F32)
        total = got_ref[:, at].astype(F32)
        step = 1
        while step < count:
            keep = row >= step
            total = total + decay * jnp.where(keep, pltpu.roll(total, step, 0), 0.0)
            decay = decay * jnp.where(keep, pltpu.roll(decay, step, 0), 1.0)
            step *= 2
        out_ref[:, at] = jnp.where(row >= 1, pltpu.roll(total, 1, 0), 0.0).astype(BF16)


def local_kernel(chunks, *refs):
    x_ref, maps_ref, step_ref, sums_ref, skip_ref = refs[:5]
    y_ref, state_scr = refs[-2:]
    state_scr[...] = jnp.zeros_like(state_scr)
    jdx = lax.broadcasted_iota(jnp.int32, (CHUNK, CHUNK), 0)
    idx = lax.broadcasted_iota(jnp.int32, (CHUNK, CHUNK), 1)
    causal = idx >= jdx

    def chunk_body(c, carry):
        at = pl.ds(pl.multiple_of(c * CHUNK, CHUNK), CHUNK)
        keys = maps_ref[:STATE, at]
        queries = maps_ref[STATE:, at]
        affinity = jnp.dot(jnp.transpose(keys), queries, preferred_element_type=F32)
        affinity = jnp.where(causal, affinity, 0.0)
        queries32 = queries.astype(F32)
        sums = sums_ref[:, at]
        steps = step_ref[:, at]
        ends = jnp.broadcast_to(sums[:, CHUNK - 1 :], (GROUP, CHUNK))
        rise = jnp.exp2(sums)
        fall = jnp.exp2(ends - sums) * steps
        columns = jnp.transpose(jnp.log2(steps) - sums)
        scaled = []
        for h in range(GROUP):
            rows = slice(h * HEAD_DIM, (h + 1) * HEAD_DIM)
            x = x_ref[rows, at]
            x32 = x.astype(F32)
            gaps = sums[h : h + 1, :] + columns[:, h : h + 1]
            weights = (affinity * jnp.exp2(jnp.minimum(gaps, 0.0))).astype(BF16)
            risen = (queries32 * rise[h : h + 1, :]).astype(BF16)
            state = state_scr[rows, :]
            left = jnp.concatenate([x, state.astype(BF16)], axis=1)
            right = jnp.concatenate([weights, risen], axis=0)
            out = jnp.dot(left, right, preferred_element_type=F32)
            out = out + x32 * skip_ref[rows, :1]
            y_ref[rows, at] = out.astype(BF16)
            scaled.append((x32 * fall[h : h + 1, :]).astype(BF16))
        update = dot_nt(jnp.concatenate(scaled, axis=0), keys)
        for h in range(GROUP):
            rows = slice(h * HEAD_DIM, (h + 1) * HEAD_DIM)
            decay = jnp.broadcast_to(rise[h : h + 1, CHUNK - 1 :], (HEAD_DIM, STATE))
            state_scr[rows, :] = state_scr[rows, :] * decay + update[rows]
        return carry

    lax.fori_loop(0, chunks, chunk_body, 0)


def carried_kernel(chunks, y_ref, maps_ref, lead_ref, enter_ref, out_ref):
    first = jnp.transpose(enter_ref[0])
    second = jnp.transpose(enter_ref[1])
    entering = jnp.concatenate([first, second], axis=0)
    for c in range(chunks // 2):
        at = slice(c * 256, (c + 1) * 256)
        carried = jnp.dot(entering, maps_ref[STATE:, at], preferred_element_type=F32)
        for h in range(GROUP):
            rows = slice(h * HEAD_DIM, (h + 1) * HEAD_DIM)
            add = carried[rows] * lead_ref[h : h + 1, at]
            out_ref[rows, at] = (y_ref[rows, at].astype(F32) + add).astype(BF16)


def local(raw_inputs, state_maps, step_size, log_decay, conv_weight, conv_bias, skip_gain, axis):
    channels, tokens = raw_inputs.shape
    heads = skip_gain.shape[0]
    groups = heads // GROUP
    chunks = tokens // CHUNK
    count = lax.axis_size(axis)
    half = channels // 2

    tail = lax.ppermute(
        raw_inputs[:, tokens - 3 :], axis, [(i, i + 1) for i in range(count - 1)]
    )
    halo = jnp.pad(tail, ((0, 0), (CHUNK - 3, 0)))

    block = lambda g: (g, 0)
    whole = lambda g: (0, 0)
    big = pl.BlockSpec((ROWS, tokens), block)
    rows8 = pl.BlockSpec((GROUP, tokens), block)
    maps = pl.BlockSpec((2 * STATE, tokens), whole)
    cost = lambda us: pl.CostEstimate(
        flops=int(us * 5e8), bytes_accessed=int(us * 1e6), transcendentals=0
    )
    params = pltpu.CompilerParams(dimension_semantics=("arbitrary",))

    values, sums, lead, message = pl.pallas_call(
        functools.partial(values_kernel, chunks),
        grid=(groups,),
        in_specs=[
            big,
            pl.BlockSpec((ROWS, CHUNK), block),
            maps,
            rows8,
            rows8,
            pl.BlockSpec((4, ROWS), lambda g: (0, g)),
            pl.BlockSpec((1, ROWS), lambda g: (0, g)),
        ],
        out_specs=[big, rows8, rows8, pl.BlockSpec((2, STATE, half + CHUNK), lambda g: (0, 0, 0))],
        out_shape=[
            jax.ShapeDtypeStruct((channels, tokens), BF16),
            jax.ShapeDtypeStruct((heads, tokens), F32),
            jax.ShapeDtypeStruct((heads, tokens), F32),
            jax.ShapeDtypeStruct((2, STATE, half + CHUNK), BF16),
        ],
        scratch_shapes=[
            pltpu.VMEM((ROWS, 8), F32),
            pltpu.VMEM((GROUP, 8, tokens), F32),
            pltpu.VMEM((128, tokens), BF16),
            pltpu.VMEM((GROUP, CHUNK), F32),
        ],
        compiler_params=params,
        cost_estimate=cost(20),
        name="values",
    )(raw_inputs, halo, state_maps, step_size, log_decay, conv_weight, conv_bias.reshape(1, channels))

    got = lax.all_to_all(message.reshape(2 * STATE, half + CHUNK), axis, 0, 0, tiled=True)

    skip = jnp.broadcast_to(jnp.repeat(skip_gain, HEAD_DIM)[:, None], (channels, 128))

    def local_part(first, number, previous):
        shift = lambda g: (g + first, 0)
        specs = [
            pl.BlockSpec((ROWS, tokens), shift),
            maps,
            pl.BlockSpec((GROUP, tokens), shift),
            pl.BlockSpec((GROUP, tokens), shift),
            pl.BlockSpec((ROWS, 128), shift),
        ]
        arrays = [values, state_maps, step_size, sums, skip]
        alias = {}
        if previous is not None:
            specs.append(pl.BlockSpec(memory_space=pl.ANY))
            arrays.append(previous)
            alias = {5: 0}
        return pl.pallas_call(
            functools.partial(local_kernel, chunks),
            grid=(number,),
            in_specs=specs,
            out_specs=pl.BlockSpec((ROWS, tokens), shift),
            out_shape=jax.ShapeDtypeStruct((channels, tokens), BF16),
            scratch_shapes=[pltpu.VMEM((ROWS, STATE), F32)],
            input_output_aliases=alias,
            compiler_params=params,
            cost_estimate=cost(4 * number),
            name="inside",
        )(*arrays)

    early = groups // 2
    partial = local_part(0, early, None)

    entering = pl.pallas_call(
        scan_kernel,
        in_specs=[pl.BlockSpec(memory_space=pltpu.VMEM)],
        out_specs=pl.BlockSpec(memory_space=pltpu.VMEM),
        out_shape=jax.ShapeDtypeStruct((count, half), BF16),
        cost_estimate=cost(3),
        name="scan",
    )(got)
    back = lax.all_to_all(entering, axis, 0, 0, tiled=True).reshape(2, STATE, half)

    partial = local_part(early, groups - early, partial)

    return pl.pallas_call(
        functools.partial(carried_kernel, chunks),
        grid=(groups,),
        in_specs=[
            big,
            maps,
            rows8,
            pl.BlockSpec((2, STATE, 4 * HEAD_DIM), lambda g: (0, 0, g)),
        ],
        out_specs=big,
        out_shape=jax.ShapeDtypeStruct((channels, tokens), BF16),
        input_output_aliases={0: 0},
        compiler_params=params,
        cost_estimate=cost(8),
        name="carried",
    )(partial, state_maps, lead, back)


def solution(mesh):
    axis = mesh.axis_names[0]
    return jax.shard_map(
        functools.partial(local, axis=axis),
        mesh=mesh,
        in_specs=(P(None, axis),) * 4 + (P(),) * 3,
        out_specs=P(None, axis),
        check_vma=False,
    )
```

profile of v0, /device:TPU:1, one launch (start us, length us, event | category | flops | bytes accessed | tf_op | source)
XLA Modules:
  0.0 156.2 jit_solution(1432761936377139908)
XLA Ops:
  0.0 1.5 slice.3
  1.5 0.3 copy.20
  1.8 4.9 %collective-permute-start = (bf16[3584,3]{0,1:T(4,128)(2,1)S(1)}, bf16[3584,3]{0,1:T(4,128)(2,1)S(1)}, u32[]{:S(2)}, u32[]{:S(2)}) collective-permute-start(bf16[3584,3]{0,1:T(4,128)(2,1)S(1)} %copy.20), channel_id=1, source_target_pairs={{0,1},{1,2},{2,3},{3,4},{4,5},{5,6},{6,7},{7,8},{8,9},{9,10},{10,1... | collective-permute-start | bytes 64520 | tf_op jit(solution)/shard_map/ppermute | solution.py:211
  6.8 1.3 reshape.14.bias_ref
  8.1 0.7 broadcast_in_dim.10
  8.8 0.1 broadcast_in_dim.11
  8.9 0.0 collective-permute-done
  8.9 0.5 copy.15
  9.4 1.3 pad.4.halo_ref
  10.6 38.5 %values.1 = (bf16[3584,1792]{1,0:T(8,128)(2,1)}, f32[56,1792]{1,0:T(8,128)}, f32[56,1792]{1,0:T(8,128)}, bf16[2,64,1920]{2,1,0:T(8,128)(2,1)}) custom-call(bf16[3584,1792]{1,0:T(8,128)(2,1)} %raw_ref.1, bf16[3584,128]{1,0:T(8,128)(2,1)} %pad.4.halo_ref, bf16[128,1792]{1,0:T(8,128)(2,1)} %maps_ref.3, f32[56,1792]{1,0:T(8,128)} %refs_2_.3, ...), custom_call_target="tpu_custom_call" | custom-call | flops 10000000000 | bytes 20000000 | tf_op jit(solution)/shard_map/values/pallas_call | solution.py:226
  49.2 0.5 broadcast.2
  49.7 1.9 %reduce = bf16[128,1920]{1,0:T(8,128)(2,1)S(1)} reduce(bf16[128,1,1920]{2,0,1:T(8,128)(2,1)} %bitcast.7, bf16[]{:T(256)} %broadcast.2), dimensions={1}, to_apply=%copy.16.reduce_sub_computation | reduce | bytes 983042 | tf_op jit(solution)/shard_map/all_to_all | solution.py:256
  51.5 1.3 reshape.16
  52.8 9.6 %all-to-all-start = ((bf16[128,2,960]{2,1,0:T(2,128)(2,1)}), bf16[128,2,960]{2,1,0:T(2,128)(2,1)S(1)}, u32[]{:S(2)}, u32[]{:S(2)}) async-start(bf16[128,2,960]{2,1,0:T(2,128)(2,1)} %reshape.16), calls=%async_computation | async-start | bytes 1048576 | tf_op jit(solution)/shard_map/all_to_all | solution.py:256
  62.5 1.8 %broadcast_in_dim.12.refs_4_ = f32[3584,128]{1,0:T(8,128)} broadcast(f32[3584]{0:T(1024)S(1)} %broadcast_in_dim.11), dimensions={0} | broadcast | bytes 1849344 | tf_op jit(solution)/shard_map/broadcast_in_dim | solution.py:258
  64.3 26.2 %inside.2.refs_5_ = bf16[3584,1792]{1,0:T(8,128)(2,1)} custom-call(bf16[3584,1792]{1,0:T(8,128)(2,1)} %get-tuple-element.9.refs_0_, bf16[128,1792]{1,0:T(8,128)(2,1)} %maps_ref.3, f32[56,1792]{1,0:T(8,128)} %refs_2_.3, f32[56,1792]{1,0:T(8,128)} %get-tuple-element.10.refs_3_, f32[3584,128]{1,0:T(8,128)} %broadcast_in_dim.12.refs_4_), custom_call_target="tpu_custom_call" | custom-call | flops 6000000000 | bytes 12000000 | tf_op jit(solution)/shard_map/inside/pallas_call | solution.py:275
  90.5 0.0 all-to-all-done
  90.5 0.7 reshape.17
  91.2 0.9 copy.22
  92.0 3.1 %scan.1 = bf16[128,1792]{1,0:T(8,128)(2,1)} custom-call(bf16[128,1920]{1,0:T(8,128)(2,1)} %bitcast.8), custom_call_target="tpu_custom_call" | custom-call | flops 1500000000 | bytes 3000000 | tf_op jit(solution)/shard_map/scan/pallas_call | solution.py:291
  95.1 1.8 %reduce.1 = bf16[128,1792]{1,0:T(8,128)(2,1)S(1)} reduce(bf16[128,1,1792]{2,0,1:T(8,128)(2,1)} %bitcast.9, bf16[]{:T(256)} %broadcast.2), dimensions={1}, to_apply=%copy.17.reduce_sub_computation | reduce | bytes 917506 | tf_op jit(solution)/shard_map/all_to_all | solution.py:299
  97.0 0.9 reshape.18
  97.9 9.8 %all-to-all-start.1 = ((bf16[128,2,896]{2,1,0:T(2,128)(2,1)}), bf16[128,2,896]{2,1,0:T(2,128)(2,1)S(1)}, u32[]{:S(2)}, u32[]{:S(2)}) async-start(bf16[128,2,896]{2,1,0:T(2,128)(2,1)} %reshape.18), calls=%async_computation.1 | async-start | bytes 917504 | tf_op jit(solution)/shard_map/all_to_all | solution.py:299
  107.6 33.2 %inside.3.y_ref = bf16[3584,1792]{1,0:T(8,128)(2,1)} custom-call(bf16[3584,1792]{1,0:T(8,128)(2,1)} %get-tuple-element.9.refs_0_, bf16[128,1792]{1,0:T(8,128)(2,1)} %maps_ref.3, f32[56,1792]{1,0:T(8,128)} %refs_2_.3, f32[56,1792]{1,0:T(8,128)} %get-tuple-element.10.refs_3_, f32[3584,128]{1,0:T(8,128)} %broadcast_in_dim.12.refs_4_, ...), custom_call_target="tpu_custom_call", output_to_operand_aliasing={{}: (5, {})} | custom-call | flops 8000000000 | bytes 16000000 | tf_op jit(solution)/shard_map/inside/pallas_call | solution.py:275
  140.8 0.0 all-to-all-done.1
  140.8 0.4 reshape.19
  141.2 0.8 copy.19
  142.0 14.2 %carried.1 = bf16[3584,1792]{1,0:T(8,128)(2,1)} custom-call(bf16[3584,1792]{1,0:T(8,128)(2,1)} %inside.3.y_ref, bf16[128,1792]{1,0:T(8,128)(2,1)} %maps_ref.3, f32[56,1792]{1,0:T(8,128)} %get-tuple-element.11.lead_ref, bf16[2,64,1792]{2,1,0:T(8,128)(2,1)} %bitcast.6), custom_call_target="tpu_custom_call", output_to_operand_aliasing={{}: (0, {})} | custom-call | flops 4000000000 | bytes 8000000 | tf_op jit(solution)/shard_map/carried/pallas_call | solution.py:303
Async XLA Ops:
  1.8 7.1 %collective-permute-start = (bf16[3584,3]{0,1:T(4,128)(2,1)S(1)}, bf16[3584,3]{0,1:T(4,128)(2,1)S(1)}, u32[]{:S(2)}, u32[]{:S(2)}) collective-permute-start(bf16[3584,3]{0,1:T(4,128)(2,1)S(1)} %copy.20), channel_id=1, source_target_pairs={{0,1},{1,2},{2,3},{3,4},{4,5},{5,6},{6,7},{7,8},{8,9},{9,10},{10,1... | collective-permute-start | bytes 64520 | tf_op jit(solution)/shard_map/ppermute | solution.py:211
  52.8 37.6 %all-to-all-start = ((bf16[128,2,960]{2,1,0:T(2,128)(2,1)}), bf16[128,2,960]{2,1,0:T(2,128)(2,1)S(1)}, u32[]{:S(2)}, u32[]{:S(2)}) async-start(bf16[128,2,960]{2,1,0:T(2,128)(2,1)} %reshape.16), calls=%async_computation | async-start | bytes 1048576 | tf_op jit(solution)/shard_map/all_to_all | solution.py:256
  97.9 43.0 %all-to-all-start.1 = ((bf16[128,2,896]{2,1,0:T(2,128)(2,1)}), bf16[128,2,896]{2,1,0:T(2,128)(2,1)S(1)}, u32[]{:S(2)}, u32[]{:S(2)}) async-start(bf16[128,2,896]{2,1,0:T(2,128)(2,1)} %reshape.18), calls=%async_computation.1 | async-start | bytes 917504 | tf_op jit(solution)/shard_map/all_to_all | solution.py:299
where the time goes:
time: 157 us; the launch traced here: 156 us
  Pallas kernels  115 us (73%)
  starting transfers between devices  24.3 us (15%)
  local copies, waits for them, and re-layouts  13 us (8%)
  other arithmetic  3.7 us (2%)
    pallas_call x2, Pallas kernels, local_part(): pl.pallas_call(functools.partial(local_kernel, chunks), grid=(number,), i...  59.4 us
    pallas_call x1, Pallas kernels, local(): pl.pallas_call(functools.partial(values_kernel, chunks), grid=(groups,),...  38.5 us
    pallas_call x1, Pallas kernels, local(): pl.pallas_call(functools.partial(carried_kernel, chunks), grid=(groups,),...  14.2 us
    all_to_all x1, starting transfers between devices, local(): lax.all_to_all(entering, axis, 0, 0, tiled=True).reshape(2, STATE, half)  9.75 us
    all_to_all x1, starting transfers between devices, local(): lax.all_to_all(message.reshape(2 * STATE, half + CHUNK), axis, 0, 0, tile...  9.65 us
    unnamed x7, local copies, waits for them, and re-layouts  5.31 us
    ppermute x1, starting transfers between devices, local(): lax.ppermute(raw_inputs[:, tokens - 3:], axis, [(i, i + 1) for i in range...  4.92 us
  transfers between devices with their start and end apart: 3, of which 0 were waited for; matrix products, arithmetic and copies ran while one was open for 3% of the time, Pallas kernels for 38%

commit v1 on v0

v1 whole, which is shorter than its diff:
```python
import functools

import jax
import jax.numpy as jnp
from jax import lax
from jax.experimental import pallas as pl
from jax.experimental.pallas import tpu as pltpu
from jax.sharding import PartitionSpec as P

CHUNK = 128
SEGMENT = 16
GROUP = 8
HEAD_DIM = 64
STATE = 64
ROWS = GROUP * HEAD_DIM
LOG2E = 1.4426950408889634
F32 = jnp.float32
BF16 = jnp.bfloat16


def dot_nt(a, b):
    return lax.dot_general(a, b, (((1,), (1,)), ((), ())), preferred_element_type=F32)


def chunk_sums(log_decay, chunks):
    stacked = jnp.concatenate(
        [log_decay[:, c * CHUNK : (c + 1) * CHUNK] for c in range(chunks)], axis=0
    ) * LOG2E
    row = lax.broadcasted_iota(jnp.int32, (CHUNK, CHUNK), 0)
    col = lax.broadcasted_iota(jnp.int32, (CHUNK, CHUNK), 1)
    upper = jnp.where(row <= col, 1.0, 0.0).astype(F32)
    summed = lax.dot_general(
        stacked, upper, (((1,), (0,)), ((), ())),
        precision=lax.Precision.HIGHEST, preferred_element_type=F32,
    )
    return [summed[c * GROUP : (c + 1) * GROUP] for c in range(chunks)]


def values_kernel(chunks, raw_ref, halo_ref, maps_ref, step_ref, decay_ref, taps_ref, bias_ref,
                  x_ref, sums_ref, lead_ref, msg_ref, d_scr, xd_scr):
    sums = chunk_sums(decay_ref[...], chunks)
    ends = [jnp.broadcast_to(s[:, CHUNK - 1 :], (GROUP, CHUNK)) for s in sums]
    before = jnp.zeros((GROUP, CHUNK), F32)
    for c in range(chunks):
        at = slice(c * CHUNK, (c + 1) * CHUNK)
        sums_ref[:, at] = sums[c]
        lead_ref[:, at] = jnp.exp2(before + sums[c])
        before = before + ends[c]
    after = jnp.zeros((GROUP, CHUNK), F32)
    for c in reversed(range(chunks)):
        at = slice(c * CHUNK, (c + 1) * CHUNK)
        to_end = jnp.exp2((ends[c] - sums[c]) + after) * step_ref[:, at]
        for h in range(GROUP):
            d_scr[h, :, at] = jnp.broadcast_to(to_end[h : h + 1, :], (8, CHUNK))
        after = after + ends[c]
    total = jnp.exp2(before)
    hi = total.astype(BF16).astype(F32)
    low = total - hi
    for h in range(GROUP):
        tile = jnp.concatenate(
            [jnp.broadcast_to(hi[h : h + 1], (8, CHUNK)), jnp.broadcast_to(low[h : h + 1], (8, CHUNK))], axis=0
        ).astype(BF16)
        msg_ref[2 * h, 16:, :] = tile
        msg_ref[2 * h + 1, 16:, :] = tile

    keys = maps_ref[:STATE, :]
    row = lax.broadcasted_iota(jnp.int32, (HEAD_DIM, 4 * HEAD_DIM), 0)
    col = lax.broadcasted_iota(jnp.int32, (HEAD_DIM, 4 * HEAD_DIM), 1)
    diagonal = row == lax.rem(col, HEAD_DIM)
    lane = lax.broadcasted_iota(jnp.int32, (HEAD_DIM, CHUNK), 1)
    inside = [lane >= k for k in range(4)]

    def head_body(head, carry):
        rows = pl.ds(pl.multiple_of(head * HEAD_DIM, HEAD_DIM), HEAD_DIM)
        taps = jnp.broadcast_to(taps_ref[head, :1, :], (HEAD_DIM, 4 * HEAD_DIM))
        taps = jnp.where(diagonal, taps, 0.0)
        taps_hi = taps.astype(BF16)
        taps_low = (taps - taps_hi.astype(F32)).astype(BF16)
        left = jnp.concatenate([taps_hi, taps_low], axis=0)
        bias = jnp.broadcast_to(bias_ref[rows, :1], (HEAD_DIM, 2 * CHUNK))
        last = halo_ref[rows, :]
        prior = [None] + [pltpu.roll(last, k, 1) for k in (1, 2, 3)]
        for t in range(chunks // 2):
            columns = []
            for c in (2 * t, 2 * t + 1):
                now = raw_ref[rows, c * CHUNK : (c + 1) * CHUNK]
                rolled = [None] + [pltpu.roll(now, k, 1) for k in (1, 2, 3)]
                moved = [jnp.where(inside[k], rolled[k], prior[k]) for k in (3, 2, 1)]
                columns.append(jnp.concatenate(moved + [now], axis=0))
                prior = rolled
            at = slice(2 * t * CHUNK, 2 * (t + 1) * CHUNK)
            both = jnp.dot(left, jnp.concatenate(columns, axis=1), preferred_element_type=F32)
            half = (both[:HEAD_DIM] + both[HEAD_DIM:]) + bias
            value = half + half * jnp.tanh(half)
            x_ref[rows, at] = value.astype(BF16)
            to_end = d_scr[head, :, at]
            to_end = jnp.concatenate([to_end] * 8, axis=0)
            xd_scr[:, at] = (value * to_end).astype(BF16)
        state = dot_nt(xd_scr[...], keys).astype(BF16)
        for k in range(2):
            msg_ref[2 * head + k, :16, :] = jnp.concatenate(
                [state[32 * k : 32 * k + 16], state[32 * k + 16 : 32 * k + 32]], axis=1
            )
        return carry

    lax.fori_loop(0, GROUP, head_body, 0)


def scan_kernel(got_ref, out_ref):
    entering = jnp.zeros((16, 128), F32)
    for d in range(got_ref.shape[0]):
        out_ref[d] = entering.astype(BF16)
        parts = got_ref[d, 16:, :].astype(F32)
        decay = parts[:8] + parts[8:]
        decay = jnp.concatenate([decay, decay], axis=0)
        entering = decay * entering + got_ref[d, :16, :].astype(F32)


def local_kernel(chunks, *refs):
    x_ref, maps_ref, step_ref, sums_ref, skip_ref = refs[:5]
    y_ref, state_scr = refs[-2:]
    state_scr[...] = jnp.zeros_like(state_scr)
    jdx = lax.broadcasted_iota(jnp.int32, (CHUNK, CHUNK), 0)
    idx = lax.broadcasted_iota(jnp.int32, (CHUNK, CHUNK), 1)
    causal = idx >= jdx
    segment = lax.div(lax.broadcasted_iota(jnp.int32, (GROUP, CHUNK), 1), SEGMENT)

    def one_chunk(c):
        at = pl.ds(pl.multiple_of(c * CHUNK, CHUNK), CHUNK)
        keys = maps_ref[:STATE, at]
        queries = maps_ref[STATE:, at]
        affinity = jnp.dot(jnp.transpose(keys), queries, preferred_element_type=F32)
        affinity = jnp.where(causal, affinity, 0.0)
        queries32 = queries.astype(F32)
        sums = sums_ref[:, at]
        steps = step_ref[:, at]
        ends = jnp.broadcast_to(sums[:, CHUNK - 1 :], (GROUP, CHUNK))
        rise = jnp.exp2(sums)
        fall = jnp.exp2(ends - sums) * steps
        marks = ends
        grown = []
        for b in range(CHUNK // SEGMENT):
            last = (b + 1) * SEGMENT - 1
            mark = jnp.broadcast_to(sums[:, last : last + 1], (GROUP, CHUNK))
            grown.append(jnp.exp2(jnp.minimum(sums - mark, 100.0)))
            marks = jnp.where(segment == b, mark, marks)
        shrunk = jnp.exp2(marks - sums) * steps
        scaled = []
        for h in range(GROUP):
            rows = slice(h * HEAD_DIM, (h + 1) * HEAD_DIM)
            x = x_ref[rows, at]
            x32 = x.astype(F32)
            pieces = [
                affinity[b * SEGMENT : (b + 1) * SEGMENT] * grown[b][h : h + 1, :]
                for b in range(CHUNK // SEGMENT)
            ]
            weights = jnp.concatenate(pieces, axis=0).astype(BF16)
            risen = (queries32 * rise[h : h + 1, :]).astype(BF16)
            stepped = (x32 * shrunk[h : h + 1, :]).astype(BF16)
            state = state_scr[rows, :]
            left = jnp.concatenate([stepped, state.astype(BF16)], axis=1)
            right = jnp.concatenate([weights, risen], axis=0)
            out = jnp.dot(left, right, preferred_element_type=F32)
            out = out + x32 * skip_ref[rows, :1]
            y_ref[rows, at] = out.astype(BF16)
            scaled.append((x32 * fall[h : h + 1, :]).astype(BF16))
        update = dot_nt(jnp.concatenate(scaled, axis=0), keys)
        for h in range(GROUP):
            rows = slice(h * HEAD_DIM, (h + 1) * HEAD_DIM)
            decay = jnp.broadcast_to(rise[h : h + 1, CHUNK - 1 :], (HEAD_DIM, STATE))
            state_scr[rows, :] = state_scr[rows, :] * decay + update[rows]

    def body(t, carry):
        for k in range(2):
            one_chunk(2 * t + k)
        return carry

    lax.fori_loop(0, chunks // 2, body, 0)


def carried_kernel(chunks, y_ref, maps_ref, lead_ref, enter_ref, out_ref):
    for c in range(chunks // 2):
        at = slice(c * 256, (c + 1) * 256)
        queries = maps_ref[STATE:, at]
        pieces = []
        for h in range(2 * GROUP):
            tile = enter_ref[h]
            pieces += [tile[:, :STATE], tile[:, STATE:]]
        entering = jnp.concatenate(pieces, axis=0)
        carried = jnp.dot(entering, queries, preferred_element_type=F32)
        for h in range(GROUP):
            rows = slice(h * HEAD_DIM, (h + 1) * HEAD_DIM)
            add = carried[rows] * lead_ref[h : h + 1, at]
            out_ref[rows, at] = (y_ref[rows, at].astype(F32) + add).astype(BF16)


def local(raw_inputs, state_maps, step_size, log_decay, conv_weight, conv_bias, skip_gain, axis):
    channels, tokens = raw_inputs.shape
    heads = skip_gain.shape[0]
    groups = heads // GROUP
    chunks = tokens // CHUNK
    count = lax.axis_size(axis)

    tail = lax.ppermute(
        raw_inputs[:, tokens - 3 :], axis, [(i, i + 1) for i in range(count - 1)]
    )
    halo = jnp.pad(tail, ((0, 0), (CHUNK - 3, 0)))

    taps = 0.5 * jnp.transpose(conv_weight.reshape(4, heads, HEAD_DIM), (1, 0, 2))
    taps = taps.reshape(heads, 1, 4 * HEAD_DIM)
    bias = jnp.broadcast_to(0.5 * conv_bias[:, None], (channels, 128))

    block = lambda g: (g, 0)
    whole = lambda g: (0, 0)
    big = pl.BlockSpec((ROWS, tokens), block)
    rows8 = pl.BlockSpec((GROUP, tokens), block)
    maps = pl.BlockSpec((2 * STATE, tokens), whole)
    cost = lambda us: pl.CostEstimate(
        flops=int(us * 5e8), bytes_accessed=int(us * 1e6), transcendentals=0
    )
    params = pltpu.CompilerParams(dimension_semantics=("arbitrary",))

    values, sums, lead, message = pl.pallas_call(
        functools.partial(values_kernel, chunks),
        grid=(groups,),
        in_specs=[
            big,
            pl.BlockSpec((ROWS, CHUNK), block),
            maps,
            rows8,
            rows8,
            pl.BlockSpec((GROUP, 1, 4 * HEAD_DIM), lambda g: (g, 0, 0)),
            pl.BlockSpec((ROWS, 128), block),
        ],
        out_specs=[big, rows8, rows8, pl.BlockSpec((2 * GROUP, 32, 128), lambda g: (g, 0, 0))],
        out_shape=[
            jax.ShapeDtypeStruct((channels, tokens), BF16),
            jax.ShapeDtypeStruct((heads, tokens), F32),
            jax.ShapeDtypeStruct((heads, tokens), F32),
            jax.ShapeDtypeStruct((count, 32, 128), BF16),
        ],
        scratch_shapes=[
            pltpu.VMEM((GROUP, 8, tokens), F32),
            pltpu.VMEM((HEAD_DIM, tokens), BF16),
        ],
        compiler_params=params,
        cost_estimate=cost(20),
        name="values",
    )(raw_inputs, halo, state_maps, step_size, log_decay, taps, bias)

    got = lax.all_to_all(message, axis, 0, 0, tiled=True)

    skip = jnp.broadcast_to(jnp.repeat(skip_gain, HEAD_DIM)[:, None], (channels, 128))

    def local_part(first, number, previous):
        shift = lambda g: (g + first, 0)
        specs = [
            pl.BlockSpec((ROWS, tokens), shift),
            maps,
            pl.BlockSpec((GROUP, tokens), shift),
            pl.BlockSpec((GROUP, tokens), shift),
            pl.BlockSpec((ROWS, 128), shift),
        ]
        arrays = [values, state_maps, step_size, sums, skip]
        alias = {}
        if previous is not None:
            specs.append(pl.BlockSpec(memory_space=pl.ANY))
            arrays.append(previous)
            alias = {5: 0}
        return pl.pallas_call(
            functools.partial(local_kernel, chunks),
            grid=(number,),
            in_specs=specs,
            out_specs=pl.BlockSpec((ROWS, tokens), shift),
            out_shape=jax.ShapeDtypeStruct((channels, tokens), BF16),
            scratch_shapes=[pltpu.VMEM((ROWS, STATE), F32)],
            input_output_aliases=alias,
            compiler_params=params,
            cost_estimate=cost(4 * number),
            name="inside",
        )(*arrays)

    early = groups // 2
    partial = local_part(0, early, None)

    entering = pl.pallas_call(
        scan_kernel,
        in_specs=[pl.BlockSpec(memory_space=pltpu.VMEM)],
        out_specs=pl.BlockSpec(memory_space=pltpu.VMEM),
        out_shape=jax.ShapeDtypeStruct((count, 16, 128), BF16),
        cost_estimate=cost(3),
        name="scan",
    )(got)
    back = lax.all_to_all(entering, axis, 0, 0, tiled=True)

    partial = local_part(early, groups - early, partial)

    return pl.pallas_call(
        functools.partial(carried_kernel, chunks),
        grid=(groups,),
        in_specs=[
            big,
            maps,
            rows8,
            pl.BlockSpec((2 * GROUP, 16, 128), lambda g: (g, 0, 0)),
        ],
        out_specs=big,
        out_shape=jax.ShapeDtypeStruct((channels, tokens), BF16),
        input_output_aliases={0: 0},
        compiler_params=params,
        cost_estimate=cost(8),
        name="carried",
    )(partial, state_maps, lead, back)


def solution(mesh):
    axis = mesh.axis_names[0]
    return jax.shard_map(
        functools.partial(local, axis=axis),
        mesh=mesh,
        in_specs=(P(None, axis),) * 4 + (P(),) * 3,
        out_specs=P(None, axis),
        check_vma=False,
    )
```

time: 157 us -> 142 us (0.904)
  Pallas kernels: 115 us -> 105 us
  local copies, waits for them, and re-layouts: 13 us -> 10 us
  other arithmetic: 3.7 us -> 1.56 us
    pallas_call x2, Pallas kernels: 59.4 us -> 48 us  [local_part(): pl.pallas_call(functools.partial(local_kernel, chunks), grid=(number,), i...]
    all_to_all x2 -> x0, other arithmetic: 3.7 us -> none  [the longest x1 1.86 us: local(): lax.all_to_all(message.reshape(2 * STATE, half + CHUNK), axis, 0, 0, tile...]
    unnamed x7, local copies, waits for them, and re-layouts: 5.31 us -> 2.13 us
    pallas_call x1, Pallas kernels: 38.5 us -> 41 us  [local(): pl.pallas_call(functools.partial(values_kernel, chunks), grid=(groups,),...]
    broadcast_in_dim x0 -> x1, local copies, waits for them, and re-layouts: none -> 1.77 us  [local(): bias = jnp.broadcast_to(0.5 * conv_bias[:, None], (channels, 128))]
  transfers between devices with their start and end apart: 3 -> 3, of which waited for: 0 -> 0; matrix products, arithmetic and copies ran while one was open for 3% -> 3% of each run, Pallas kernels for 38% -> 34%
where the time goes in v1:
time: 142 us; the launch traced here: 141 us
  Pallas kernels  105 us (74%)
  starting transfers between devices  24.3 us (17%)
  local copies, waits for them, and re-layouts  10 us (7%)
  other arithmetic  1.56 us (1%)
    pallas_call x2, Pallas kernels, local_part(): pl.pallas_call(functools.partial(local_kernel, chunks), grid=(number,), i...  48 us
    pallas_call x1, Pallas kernels, local(): pl.pallas_call(functools.partial(values_kernel, chunks), grid=(groups,),...  41 us
    pallas_call x1, Pallas kernels, local(): pl.pallas_call(functools.partial(carried_kernel, chunks), grid=(groups,),...  14.2 us
    all_to_all x1, starting transfers between devices, local(): back = lax.all_to_all(entering, axis, 0, 0, tiled=True)  9.75 us
    all_to_all x1, starting transfers between devices, local(): got = lax.all_to_all(message, axis, 0, 0, tiled=True)  9.66 us
    ppermute x1, starting transfers between devices, local(): lax.ppermute(raw_inputs[:, tokens - 3:], axis, [(i, i + 1) for i in range...  4.92 us
  transfers between devices with their start and end apart: 3, of which 0 were waited for; matrix products, arithmetic and copies ran while one was open for 3% of the time, Pallas kernels for 34%

profile of v1, /device:TPU:1, one launch (start us, length us, event | category | flops | bytes accessed | tf_op | source)
XLA Modules:
  0.0 141.4 jit_solution(3061597925013428519)
XLA Ops:
  0.0 1.5 %slice.3 = bf16[3584,3]{1,0:T(8,128)(2,1)S(1)} slice(bf16[3584,1792]{1,0:T(8,128)(2,1)} %raw_ref.1), slice={[0:3584], [1789:1792]} | slice | bytes 43008 | tf_op jit(solution)/shard_map/slice | solution.py:205
  1.5 0.3 copy.14
  1.8 4.9 %collective-permute-start = (bf16[3584,3]{0,1:T(4,128)(2,1)S(1)}, bf16[3584,3]{0,1:T(4,128)(2,1)S(1)}, u32[]{:S(2)}, u32[]{:S(2)}) collective-permute-start(bf16[3584,3]{0,1:T(4,128)(2,1)S(1)} %copy.14), channel_id=1, source_target_pairs={{0,1},{1,2},{2,3},{3,4},{4,5},{5,6},{6,7},{7,8},{8,9},{9,10},{10,1... | collective-permute-start | bytes 64520 | tf_op jit(solution)/shard_map/ppermute | solution.py:204
  6.8 0.8 broadcast_multiply_fusion
  7.6 0.7 broadcast_multiply_fusion.1
  8.3 0.1 mul.21
  8.5 0.8 reshape.9.taps_ref
  9.2 0.0 collective-permute-done
  9.2 0.5 copy.12
  9.7 1.3 pad.4.halo_ref
  11.0 1.8 %broadcast_in_dim.16.bias_ref = f32[3584,128]{1,0:T(8,128)} broadcast(f32[3584]{0:T(1024)S(1)} %broadcast_multiply_fusion.1), dimensions={0} | broadcast | bytes 1849344 | tf_op jit(solution)/shard_map/broadcast_in_dim | solution.py:211
  12.8 0.0 copy-start.2
  12.8 41.0 %values.1 = (bf16[3584,1792]{1,0:T(8,128)(2,1)}, f32[56,1792]{1,0:T(8,128)}, f32[56,1792]{1,0:T(8,128)}, bf16[128,32,128]{2,1,0:T(8,128)(2,1)}) custom-call(bf16[3584,1792]{1,0:T(8,128)(2,1)} %raw_ref.1, bf16[3584,128]{1,0:T(8,128)(2,1)} %pad.4.halo_ref, bf16[128,1792]{1,0:T(8,128)(2,1)} %maps_ref.3, f32[56,1792]{1,0:T(8,128)} %refs_2_.3, ...), custom_call_target="tpu_custom_call" | custom-call | flops 10000000000 | bytes 20000000 | tf_op jit(solution)/shard_map/values/pallas_call | solution.py:223
  53.8 9.7 %all-to-all-start = ((bf16[128,32,128]{2,1,0:T(8,128)(2,1)}), bf16[128,32,128]{2,1,0:T(8,128)(2,1)S(1)}, u32[]{:S(2)}, u32[]{:S(2)}) async-start(bf16[128,32,128]{2,1,0:T(8,128)(2,1)} %get-tuple-element.12), calls=%async_computation | async-start | bytes 2097152 | tf_op jit(solution)/shard_map/all_to_all | solution.py:251
  63.5 0.0 copy-done.2
  63.5 0.1 broadcast_in_dim.17
  63.6 0.1 broadcast_in_dim.18
  63.7 1.8 %broadcast_in_dim.19.refs_4_ = f32[3584,128]{1,0:T(8,128)} broadcast(f32[3584]{0:T(1024)S(1)} %broadcast_in_dim.18), dimensions={0} | broadcast | bytes 1849344 | tf_op jit(solution)/shard_map/broadcast_in_dim | solution.py:253
  65.4 21.3 %inside.2.refs_5_ = bf16[3584,1792]{1,0:T(8,128)(2,1)} custom-call(bf16[3584,1792]{1,0:T(8,128)(2,1)} %get-tuple-element.9.refs_0_, bf16[128,1792]{1,0:T(8,128)(2,1)} %maps_ref.3, f32[56,1792]{1,0:T(8,128)} %refs_2_.3, f32[56,1792]{1,0:T(8,128)} %get-tuple-element.10.refs_3_, f32[3584,128]{1,0:T(8,128)} %broadcast_in_dim.19.refs_4_), custom_call_target="tpu_custom_call" | custom-call | flops 6000000000 | bytes 12000000 | tf_op jit(solution)/shard_map/inside/pallas_call | solution.py:270
  86.7 0.0 all-to-all-done.got_ref
  86.7 0.0 copy-start.1
  86.7 1.0 copy-done.1
  87.7 2.3 %scan.1 = bf16[128,16,128]{2,1,0:T(8,128)(2,1)} custom-call(bf16[128,32,128]{2,1,0:T(8,128)(2,1)} %copy-done.1), custom_call_target="tpu_custom_call" | custom-call | flops 1500000000 | bytes 3000000 | tf_op jit(solution)/shard_map/scan/pallas_call | solution.py:286
  90.0 9.8 %all-to-all-start.1 = ((bf16[128,16,128]{2,1,0:T(8,128)(2,1)}), bf16[128,16,128]{2,1,0:T(8,128)(2,1)S(1)}, u32[]{:S(2)}, u32[]{:S(2)}) async-start(bf16[128,16,128]{2,1,0:T(8,128)(2,1)} %scan.1), calls=%async_computation.1 | async-start | bytes 1048576 | tf_op jit(solution)/shard_map/all_to_all | solution.py:294
  99.8 26.7 %inside.3.y_ref = bf16[3584,1792]{1,0:T(8,128)(2,1)} custom-call(bf16[3584,1792]{1,0:T(8,128)(2,1)} %get-tuple-element.9.refs_0_, bf16[128,1792]{1,0:T(8,128)(2,1)} %maps_ref.3, f32[56,1792]{1,0:T(8,128)} %refs_2_.3, f32[56,1792]{1,0:T(8,128)} %get-tuple-element.10.refs_3_, f32[3584,128]{1,0:T(8,128)} %broadcast_in_dim.19.refs_4_, ...), custom_call_target="tpu_custom_call", output_to_operand_aliasing={{}: (5, {})} | custom-call | flops 8000000000 | bytes 16000000 | tf_op jit(solution)/shard_map/inside/pallas_call | solution.py:270
  126.4 0.0 all-to-all-done.1.enter_ref
  126.4 0.0 copy-start
  126.5 0.8 copy-done
  127.3 14.2 %carried.1 = bf16[3584,1792]{1,0:T(8,128)(2,1)} custom-call(bf16[3584,1792]{1,0:T(8,128)(2,1)} %inside.3.y_ref, bf16[128,1792]{1,0:T(8,128)(2,1)} %maps_ref.3, f32[56,1792]{1,0:T(8,128)} %get-tuple-element.11.lead_ref, bf16[128,16,128]{2,1,0:T(8,128)(2,1)} %copy-done), custom_call_target="tpu_custom_call", output_to_operand_aliasing={{}: (0, {})} | custom-call | flops 4000000000 | bytes 8000000 | tf_op jit(solution)/shard_map/carried/pallas_call | solution.py:298
  (1 shorter events, 0.0 us)
Async XLA Ops:
  1.8 7.4 %collective-permute-start = (bf16[3584,3]{0,1:T(4,128)(2,1)S(1)}, bf16[3584,3]{0,1:T(4,128)(2,1)S(1)}, u32[]{:S(2)}, u32[]{:S(2)}) collective-permute-start(bf16[3584,3]{0,1:T(4,128)(2,1)S(1)} %copy.14), channel_id=1, source_target_pairs={{0,1},{1,2},{2,3},{3,4},{4,5},{5,6},{6,7},{7,8},{8,9},{9,10},{10,1... | collective-permute-start | bytes 64520 | tf_op jit(solution)/shard_map/ppermute | solution.py:204
  12.8 50.7 %copy-start.2 = (f32[56]{0:T(128)S(1)}, f32[56]{0:T(128)}, u32[]{:S(2)}) copy-start(f32[56]{0:T(128)} %param.13) | copy-start | bytes 676
  53.8 32.9 %all-to-all-start = ((bf16[128,32,128]{2,1,0:T(8,128)(2,1)}), bf16[128,32,128]{2,1,0:T(8,128)(2,1)S(1)}, u32[]{:S(2)}, u32[]{:S(2)}) async-start(bf16[128,32,128]{2,1,0:T(8,128)(2,1)} %get-tuple-element.12), calls=%async_computation | async-start | bytes 2097152 | tf_op jit(solution)/shard_map/all_to_all | solution.py:251
  86.7 1.0 copy-start.1
  90.0 36.4 %all-to-all-start.1 = ((bf16[128,16,128]{2,1,0:T(8,128)(2,1)}), bf16[128,16,128]{2,1,0:T(8,128)(2,1)S(1)}, u32[]{:S(2)}, u32[]{:S(2)}) async-start(bf16[128,16,128]{2,1,0:T(8,128)(2,1)} %scan.1), calls=%async_computation.1 | async-start | bytes 1048576 | tf_op jit(solution)/shard_map/all_to_all | solution.py:294
  126.4 0.8 copy-start

commit v2 on v1

--- a/solution.py
+++ b/solution.py
@@ -10,6 +10,10 @@
 CHUNK = 128
 SEGMENT = 16
 GROUP = 8
+UNROLL = 8
+CHUNKS_PER_STEP = 14
+EARLY = 2
+MIDDLE = 2
 HEAD_DIM = 64
 STATE = 64
 ROWS = GROUP * HEAD_DIM
@@ -70,7 +74,7 @@
     lane = lax.broadcasted_iota(jnp.int32, (HEAD_DIM, CHUNK), 1)
     inside = [lane >= k for k in range(4)]
 
-    def head_body(head, carry):
+    def one_head(head):
         rows = pl.ds(pl.multiple_of(head * HEAD_DIM, HEAD_DIM), HEAD_DIM)
         taps = jnp.broadcast_to(taps_ref[head, :1, :], (HEAD_DIM, 4 * HEAD_DIM))
         taps = jnp.where(diagonal, taps, 0.0)
@@ -95,15 +99,19 @@
             x_ref[rows, at] = value.astype(BF16)
             to_end = d_scr[head, :, at]
             to_end = jnp.concatenate([to_end] * 8, axis=0)
-            xd_scr[:, at] = (value * to_end).astype(BF16)
-        state = dot_nt(xd_scr[...], keys).astype(BF16)
-        for k in range(2):
-            msg_ref[2 * head + k, :16, :] = jnp.concatenate(
-                [state[32 * k : 32 * k + 16], state[32 * k + 16 : 32 * k + 32]], axis=1
-            )
+            xd_scr[rows, at] = (value * to_end).astype(BF16)
+
+    def body(pair, carry):
+        for k in range(UNROLL):
+            one_head(pair * UNROLL + k)
         return carry
 
-    lax.fori_loop(0, GROUP, head_body, 0)
+    lax.fori_loop(0, GROUP // UNROLL, body, 0)
+    states = dot_nt(xd_scr[...], keys).astype(BF16)
+    for k in range(2 * GROUP):
+        msg_ref[k, :16, :] = jnp.concatenate(
+            [states[32 * k : 32 * k + 16], states[32 * k + 16 : 32 * k + 32]], axis=1
+        )
 
 
 def scan_kernel(got_ref, out_ref):
@@ -116,22 +124,37 @@
         entering = decay * entering + got_ref[d, :16, :].astype(F32)
 
 
-def local_kernel(chunks, *refs):
+def head_states(enter_ref):
+    pieces = []
+    for k in range(2 * GROUP):
+        tile = enter_ref[k]
+        pieces += [tile[:, :STATE], tile[:, STATE:]]
+    return jnp.concatenate(pieces, axis=0)
+
+
+def spread(row, count):
+    return jnp.concatenate([jnp.broadcast_to(row, (16, CHUNK)).astype(BF16)] * count, axis=0)
+
+
+def local_kernel(chunks, started, *refs):
     x_ref, maps_ref, step_ref, sums_ref, skip_ref = refs[:5]
     y_ref, state_scr = refs[-2:]
-    state_scr[...] = jnp.zeros_like(state_scr)
+    if started:
+        state_scr[...] = head_states(refs[5]).astype(F32)
+    else:
+        state_scr[...] = jnp.zeros_like(state_scr)
     jdx = lax.broadcasted_iota(jnp.int32, (CHUNK, CHUNK), 0)
     idx = lax.broadcasted_iota(jnp.int32, (CHUNK, CHUNK), 1)
     causal = idx >= jdx
     segment = lax.div(lax.broadcasted_iota(jnp.int32, (GROUP, CHUNK), 1), SEGMENT)
+    segments = CHUNK // SEGMENT
 
     def one_chunk(c):
         at = pl.ds(pl.multiple_of(c * CHUNK, CHUNK), CHUNK)
         keys = maps_ref[:STATE, at]
         queries = maps_ref[STATE:, at]
         affinity = jnp.dot(jnp.transpose(keys), queries, preferred_element_type=F32)
-        affinity = jnp.where(causal, affinity, 0.0)
-        queries32 = queries.astype(F32)
+        affinity = jnp.where(causal, affinity, 0.0).astype(BF16)
         sums = sums_ref[:, at]
         steps = step_ref[:, at]
         ends = jnp.broadcast_to(sums[:, CHUNK - 1 :], (GROUP, CHUNK))
@@ -139,7 +162,7 @@
         fall = jnp.exp2(ends - sums) * steps
         marks = ends
         grown = []
-        for b in range(CHUNK // SEGMENT):
+        for b in range(segments):
             last = (b + 1) * SEGMENT - 1
             mark = jnp.broadcast_to(sums[:, last : last + 1], (GROUP, CHUNK))
             grown.append(jnp.exp2(jnp.minimum(sums - mark, 100.0)))
@@ -148,22 +171,20 @@
         scaled = []
         for h in range(GROUP):
             rows = slice(h * HEAD_DIM, (h + 1) * HEAD_DIM)
+            one = slice(h, h + 1)
             x = x_ref[rows, at]
-            x32 = x.astype(F32)
             pieces = [
-                affinity[b * SEGMENT : (b + 1) * SEGMENT] * grown[b][h : h + 1, :]
-                for b in range(CHUNK // SEGMENT)
+                affinity[b * SEGMENT : (b + 1) * SEGMENT] * spread(grown[b][one], 1)
+                for b in range(segments)
             ]
-            weights = jnp.concatenate(pieces, axis=0).astype(BF16)
-            risen = (queries32 * rise[h : h + 1, :]).astype(BF16)
-            stepped = (x32 * shrunk[h : h + 1, :]).astype(BF16)
-            state = state_scr[rows, :]
-            left = jnp.concatenate([stepped, state.astype(BF16)], axis=1)
-            right = jnp.concatenate([weights, risen], axis=0)
+            risen = queries * spread(rise[one], 4)
+            stepped = x * spread(shrunk[one], 4)
+            left = jnp.concatenate([stepped, state_scr[rows, :].astype(BF16)], axis=1)
+            right = jnp.concatenate(pieces + [risen], axis=0)
             out = jnp.dot(left, right, preferred_element_type=F32)
-            out = out + x32 * skip_ref[rows, :1]
+            out = out + x.astype(F32) * skip_ref[one, :]
             y_ref[rows, at] = out.astype(BF16)
-            scaled.append((x32 * fall[h : h + 1, :]).astype(BF16))
+            scaled.append(x * spread(fall[one], 4))
         update = dot_nt(jnp.concatenate(scaled, axis=0), keys)
         for h in range(GROUP):
             rows = slice(h * HEAD_DIM, (h + 1) * HEAD_DIM)
@@ -171,22 +192,18 @@
             state_scr[rows, :] = state_scr[rows, :] * decay + update[rows]
 
     def body(t, carry):
-        for k in range(2):
-            one_chunk(2 * t + k)
+        for k in range(CHUNKS_PER_STEP):
+            one_chunk(CHUNKS_PER_STEP * t + k)
         return carry
 
-    lax.fori_loop(0, chunks // 2, body, 0)
+    lax.fori_loop(0, chunks // CHUNKS_PER_STEP, body, 0)
 
 
 def carried_kernel(chunks, y_ref, maps_ref, lead_ref, enter_ref, out_ref):
+    entering = head_states(enter_ref)
     for c in range(chunks // 2):
         at = slice(c * 256, (c + 1) * 256)
         queries = maps_ref[STATE:, at]
-        pieces = []
-        for h in range(2 * GROUP):
-            tile = enter_ref[h]
-            pieces += [tile[:, :STATE], tile[:, STATE:]]
-        entering = jnp.concatenate(pieces, axis=0)
         carried = jnp.dot(entering, queries, preferred_element_type=F32)
         for h in range(GROUP):
             rows = slice(h * HEAD_DIM, (h + 1) * HEAD_DIM)
@@ -241,7 +258,7 @@
         ],
         scratch_shapes=[
             pltpu.VMEM((GROUP, 8, tokens), F32),
-            pltpu.VMEM((HEAD_DIM, tokens), BF16),
+            pltpu.VMEM((ROWS, tokens), BF16),
         ],
         compiler_params=params,
         cost_estimate=cost(20),
@@ -250,25 +267,28 @@
 
     got = lax.all_to_all(message, axis, 0, 0, tiled=True)
 
-    skip = jnp.broadcast_to(jnp.repeat(skip_gain, HEAD_DIM)[:, None], (channels, 128))
-
-    def local_part(first, number, previous):
+    skip = jnp.broadcast_to(skip_gain[:, None], (heads, CHUNK))
+
+    def local_part(first, number, previous, enter=None):
         shift = lambda g: (g + first, 0)
         specs = [
             pl.BlockSpec((ROWS, tokens), shift),
             maps,
             pl.BlockSpec((GROUP, tokens), shift),
             pl.BlockSpec((GROUP, tokens), shift),
-            pl.BlockSpec((ROWS, 128), shift),
+            pl.BlockSpec((GROUP, CHUNK), shift),
         ]
         arrays = [values, state_maps, step_size, sums, skip]
         alias = {}
+        if enter is not None:
+            specs.append(pl.BlockSpec((2 * GROUP, 16, 128), lambda g: (g + first, 0, 0)))
+            arrays.append(enter)
         if previous is not None:
+            alias = {len(arrays): 0}
             specs.append(pl.BlockSpec(memory_space=pl.ANY))
             arrays.append(previous)
-            alias = {5: 0}
         return pl.pallas_call(
-            functools.partial(local_kernel, chunks),
+            functools.partial(local_kernel, chunks, enter is not None),
             grid=(number,),
             in_specs=specs,
             out_specs=pl.BlockSpec((ROWS, tokens), shift),
@@ -276,11 +296,11 @@
             scratch_shapes=[pltpu.VMEM((ROWS, STATE), F32)],
             input_output_aliases=alias,
             compiler_params=params,
-            cost_estimate=cost(4 * number),
+            cost_estimate=cost(8 * number),
             name="inside",
         )(*arrays)
 
-    early = groups // 2
+    early, middle = EARLY, EARLY + MIDDLE
     partial = local_part(0, early, None)
 
     entering = pl.pallas_call(
@@ -293,11 +313,12 @@
     )(got)
     back = lax.all_to_all(entering, axis, 0, 0, tiled=True)
 
-    partial = local_part(early, groups - early, partial)
+    partial = local_part(early, middle - early, partial)
+    partial = local_part(middle, groups - middle, partial, back)
 
     return pl.pallas_call(
         functools.partial(carried_kernel, chunks),
-        grid=(groups,),
+        grid=(middle,),
         in_specs=[
             big,
             maps,

time: 142 us -> 113 us (0.80)
  Pallas kernels: 105 us -> 74.6 us
  waiting for transfers between devices: 0.01 us -> 8.22 us
  starting transfers between devices: 24.3 us -> 19.2 us
    pallas_call x1, Pallas kernels: 41 us -> 24.2 us  [local(): pl.pallas_call(functools.partial(values_kernel, chunks), grid=(groups,),...]
    pallas_call x3 -> x4, Pallas kernels: 62.2 us -> 48 us  [the longest x3 40.2 us: local_part(): pl.pallas_call(functools.partial(local_kernel, chunks, enter is not None)...]
    all_to_all x1, waiting for transfers between devices: 0.01 us -> 6.8 us  [local(): got = lax.all_to_all(message, axis, 0, 0, tiled=True)]
    all_to_all x1, starting transfers between devices: 9.75 us -> 4.64 us  [local(): back = lax.all_to_all(entering, axis, 0, 0, tiled=True)]
  transfers between devices with their start and end apart: 3 -> 3, of which waited for: 0 -> 2; matrix products, arithmetic and copies ran while one was open for 3% -> 3% of each run, Pallas kernels for 34% -> 21%
where the time goes in v2:
time: 113 us; the launch traced here: 112 us
  Pallas kernels  74.6 us (66%)
  starting transfers between devices  19.2 us (17%)
  local copies, waits for them, and re-layouts  8.78 us (8%)
  waiting for transfers between devices  8.22 us (7%)
  other arithmetic  1.56 us (1%)
    pallas_call x3, Pallas kernels, local_part(): pl.pallas_call(functools.partial(local_kernel, chunks, enter is not None)...  40.2 us
    pallas_call x1, Pallas kernels, local(): pl.pallas_call(functools.partial(values_kernel, chunks), grid=(groups,),...  24.2 us
    all_to_all x1, starting transfers between devices, local(): got = lax.all_to_all(message, axis, 0, 0, tiled=True)  9.65 us
    pallas_call x1, Pallas kernels, local(): pl.pallas_call(functools.partial(carried_kernel, chunks), grid=(middle,),...  7.81 us
    all_to_all x1, waiting for transfers between devices, local(): got = lax.all_to_all(message, axis, 0, 0, tiled=True)  6.8 us
    ppermute x1, starting transfers between devices, local(): lax.ppermute(raw_inputs[:, tokens - 3:], axis, [(i, i + 1) for i in range...  4.92 us
    all_to_all x1, starting transfers between devices, local(): back = lax.all_to_all(entering, axis, 0, 0, tiled=True)  4.64 us
    pallas_call x1, Pallas kernels, local(): pl.pallas_call(scan_kernel, in_specs=[pl.BlockSpec(memory_space=pltpu.VME...  2.3 us
  transfers between devices with their start and end apart: 3, of which 2 were waited for; matrix products, arithmetic and copies ran while one was open for 3% of the time, Pallas kernels for 21%

profile of v2, /device:TPU:1, one launch (start us, length us, event | category | flops | bytes accessed | tf_op | source)
XLA Modules:
  0.0 112.4 jit_solution(12663716496081003122)
XLA Ops:
  0.0 1.5 %slice.3 = bf16[3584,3]{1,0:T(8,128)(2,1)S(1)} slice(bf16[3584,1792]{1,0:T(8,128)(2,1)} %raw_ref.1), slice={[0:3584], [1789:1792]} | slice | bytes 43008 | tf_op jit(solution)/shard_map/slice | solution.py:222
  1.5 0.3 copy.15
  1.8 4.9 %collective-permute-start = (bf16[3584,3]{0,1:T(4,128)(2,1)S(1)}, bf16[3584,3]{0,1:T(4,128)(2,1)S(1)}, u32[]{:S(2)}, u32[]{:S(2)}) collective-permute-start(bf16[3584,3]{0,1:T(4,128)(2,1)S(1)} %copy.15), channel_id=1, source_target_pairs={{0,1},{1,2},{2,3},{3,4},{4,5},{5,6},{6,7},{7,8},{8,9},{9,10},{10,1... | collective-permute-start | bytes 64520 | tf_op jit(solution)/shard_map/ppermute | solution.py:221
  6.8 0.8 broadcast_multiply_fusion
  7.6 0.7 broadcast_multiply_fusion.1
  8.3 0.1 mul.21
  8.5 0.7 reshape.9.taps_ref
  9.2 0.0 collective-permute-done
  9.2 0.5 copy.13
  9.7 1.3 %pad.4.halo_ref = bf16[3584,128]{1,0:T(8,128)(2,1)} pad(bf16[3584,3]{1,0:T(8,128)(2,1)S(1)} %copy.13, bf16[]{:T(256)} %constant.2.clone.1), padding=0_0x125_0 | pad | bytes 939010 | tf_op jit(solution)/shard_map/jit(_pad)/pad | solution.py:224
  10.9 1.8 %broadcast_in_dim.4.bias_ref = f32[3584,128]{1,0:T(8,128)} broadcast(f32[3584]{0:T(1024)S(1)} %broadcast_multiply_fusion.1), dimensions={0} | broadcast | bytes 1849344 | tf_op jit(solution)/shard_map/broadcast_in_dim | solution.py:228
  12.7 0.0 copy-start.2
  12.7 24.2 %values.1 = (bf16[3584,1792]{1,0:T(8,128)(2,1)}, f32[56,1792]{1,0:T(8,128)}, f32[56,1792]{1,0:T(8,128)}, bf16[128,32,128]{2,1,0:T(8,128)(2,1)}) custom-call(bf16[3584,1792]{1,0:T(8,128)(2,1)} %raw_ref.1, bf16[3584,128]{1,0:T(8,128)(2,1)} %pad.4.halo_ref, bf16[128,1792]{1,0:T(8,128)(2,1)} %maps_ref.3, f32[56,1792]{1,0:T(8,128)} %refs_2_.5, ...), custom_call_target="tpu_custom_call" | custom-call | flops 10000000000 | bytes 20000000 | tf_op jit(solution)/shard_map/values/pallas_call | solution.py:240
  37.0 9.7 %all-to-all-start = ((bf16[128,32,128]{2,1,0:T(8,128)(2,1)}), bf16[128,32,128]{2,1,0:T(8,128)(2,1)S(1)}, u32[]{:S(2)}, u32[]{:S(2)}) async-start(bf16[128,32,128]{2,1,0:T(8,128)(2,1)} %get-tuple-element.11), calls=%async_computation | async-start | bytes 2097152 | tf_op jit(solution)/shard_map/all_to_all | solution.py:268
  46.6 0.0 copy-done.2
  46.6 0.7 broadcast_in_dim.5.refs_4_
  47.3 11.7 %inside.3.refs_5_ = bf16[3584,1792]{1,0:T(8,128)(2,1)} custom-call(bf16[3584,1792]{1,0:T(8,128)(2,1)} %get-tuple-element.9.refs_0_, bf16[128,1792]{1,0:T(8,128)(2,1)} %maps_ref.3, f32[56,1792]{1,0:T(8,128)} %refs_2_.5, f32[56,1792]{1,0:T(8,128)} %get-tuple-element.10.refs_3_, f32[56,128]{1,0:T(8,128)} %broadcast_in_dim.5.refs_4_), custom_call_target="tpu_custom_call" | custom-call | flops 8000000000 | bytes 16000000 | tf_op jit(solution)/shard_map/inside/pallas_call | solution.py:290
  59.0 6.8 %all-to-all-done.got_ref = bf16[128,32,128]{2,1,0:T(8,128)(2,1)S(1)} async-done(((bf16[128,32,128]{2,1,0:T(8,128)(2,1)}), bf16[128,32,128]{2,1,0:T(8,128)(2,1)S(1)}, u32[]{:S(2)}, u32[]{:S(2)}) %all-to-all-start) | async-done | bytes 1048608 | tf_op jit(solution)/shard_map/all_to_all | solution.py:268
  65.8 0.0 copy-start.1
  65.8 1.0 copy-done.1
  66.8 2.3 %scan.1 = bf16[128,16,128]{2,1,0:T(8,128)(2,1)} custom-call(bf16[128,32,128]{2,1,0:T(8,128)(2,1)} %copy-done.1), custom_call_target="tpu_custom_call" | custom-call | flops 1500000000 | bytes 3000000 | tf_op jit(solution)/shard_map/scan/pallas_call | solution.py:306
  69.1 4.6 %all-to-all-start.1 = ((bf16[128,16,128]{2,1,0:T(8,128)(2,1)}), bf16[128,16,128]{2,1,0:T(8,128)(2,1)S(1)}, u32[]{:S(2)}, u32[]{:S(2)}) async-start(bf16[128,16,128]{2,1,0:T(8,128)(2,1)} %scan.1), calls=%async_computation.1 | async-start | bytes 1048576 | tf_op jit(solution)/shard_map/all_to_all | solution.py:314
  73.8 12.3 %inside.4.refs_6_ = bf16[3584,1792]{1,0:T(8,128)(2,1)} custom-call(bf16[3584,1792]{1,0:T(8,128)(2,1)} %get-tuple-element.9.refs_0_, bf16[128,1792]{1,0:T(8,128)(2,1)} %maps_ref.3, f32[56,1792]{1,0:T(8,128)} %refs_2_.5, f32[56,1792]{1,0:T(8,128)} %get-tuple-element.10.refs_3_, f32[56,128]{1,0:T(8,128)} %broadcast_in_dim.5.refs_4_, ...), custom_call_target="tpu_custom_call", output_to_operand_aliasing={{}: (5, {})} | custom-call | flops 8000000000 | bytes 16000000 | tf_op jit(solution)/shard_map/inside/pallas_call | solution.py:290
  86.0 1.4 %all-to-all-done.1.refs_5_.enter_ref = bf16[128,16,128]{2,1,0:T(8,128)(2,1)S(1)} async-done(((bf16[128,16,128]{2,1,0:T(8,128)(2,1)}), bf16[128,16,128]{2,1,0:T(8,128)(2,1)S(1)}, u32[]{:S(2)}, u32[]{:S(2)}) %all-to-all-start.1) | async-done | bytes 524320 | tf_op jit(solution)/shard_map/all_to_all | solution.py:314
  87.5 0.0 copy-start
  87.5 0.8 copy-done
  88.3 16.3 %inside.5.y_ref = bf16[3584,1792]{1,0:T(8,128)(2,1)} custom-call(bf16[3584,1792]{1,0:T(8,128)(2,1)} %get-tuple-element.9.refs_0_, bf16[128,1792]{1,0:T(8,128)(2,1)} %maps_ref.3, f32[56,1792]{1,0:T(8,128)} %refs_2_.5, f32[56,1792]{1,0:T(8,128)} %get-tuple-element.10.refs_3_, f32[56,128]{1,0:T(8,128)} %broadcast_in_dim.5.refs_4_, ...), custom_call_target="tpu_custom_call", output_to_operand_aliasing={{}: (6, {})} | custom-call | flops 12000000000 | bytes 24000000 | tf_op jit(solution)/shard_map/inside/pallas_call | solution.py:290
  104.6 7.8 %carried.1 = bf16[3584,1792]{1,0:T(8,128)(2,1)} custom-call(bf16[3584,1792]{1,0:T(8,128)(2,1)} %inside.5.y_ref, bf16[128,1792]{1,0:T(8,128)(2,1)} %maps_ref.3, f32[56,1792]{1,0:T(8,128)} %get-tuple-element.12.lead_ref, bf16[128,16,128]{2,1,0:T(8,128)(2,1)} %copy-done), custom_call_target="tpu_custom_call", output_to_operand_aliasing={{}: (0, {})} | custom-call | flops 4000000000 | bytes 8000000 | tf_op jit(solution)/shard_map/carried/pallas_call | solution.py:319
  (1 shorter events, 0.0 us)
Async XLA Ops:
  1.8 7.4 %collective-permute-start = (bf16[3584,3]{0,1:T(4,128)(2,1)S(1)}, bf16[3584,3]{0,1:T(4,128)(2,1)S(1)}, u32[]{:S(2)}, u32[]{:S(2)}) collective-permute-start(bf16[3584,3]{0,1:T(4,128)(2,1)S(1)} %copy.15), channel_id=1, source_target_pairs={{0,1},{1,2},{2,3},{3,4},{4,5},{5,6},{6,7},{7,8},{8,9},{9,10},{10,1... | collective-permute-start | bytes 64520 | tf_op jit(solution)/shard_map/ppermute | solution.py:221
  12.7 33.9 %copy-start.2 = (f32[56]{0:T(128)S(1)}, f32[56]{0:T(128)}, u32[]{:S(2)}) copy-start(f32[56]{0:T(128)} %param.13) | copy-start | bytes 676
  37.0 28.8 %all-to-all-start = ((bf16[128,32,128]{2,1,0:T(8,128)(2,1)}), bf16[128,32,128]{2,1,0:T(8,128)(2,1)S(1)}, u32[]{:S(2)}, u32[]{:S(2)}) async-start(bf16[128,32,128]{2,1,0:T(8,128)(2,1)} %get-tuple-element.11), calls=%async_computation | async-start | bytes 2097152 | tf_op jit(solution)/shard_map/all_to_all | solution.py:268
  65.8 1.0 copy-start.1
  69.1 18.3 %all-to-all-start.1 = ((bf16[128,16,128]{2,1,0:T(8,128)(2,1)}), bf16[128,16,128]{2,1,0:T(8,128)(2,1)S(1)}, u32[]{:S(2)}, u32[]{:S(2)}) async-start(bf16[128,16,128]{2,1,0:T(8,128)(2,1)} %scan.1), calls=%async_computation.1 | async-start | bytes 1048576 | tf_op jit(solution)/shard_map/all_to_all | solution.py:314
  87.5 0.8 copy-start

commit v3 on v2

--- a/solution.py
+++ b/solution.py
@@ -10,7 +10,6 @@
 CHUNK = 128
 SEGMENT = 16
 GROUP = 8
-UNROLL = 8
 CHUNKS_PER_STEP = 14
 EARLY = 2
 MIDDLE = 2
@@ -62,7 +61,7 @@
     low = total - hi
     for h in range(GROUP):
         tile = jnp.concatenate(
-            [jnp.broadcast_to(hi[h : h + 1], (8, CHUNK)), jnp.broadcast_to(low[h : h + 1], (8, CHUNK))], axis=0
+            [jnp.broadcast_to(hi[h : h + 1], (4, CHUNK)), jnp.broadcast_to(low[h : h + 1], (4, CHUNK))], axis=0
         ).astype(BF16)
         msg_ref[2 * h, 16:, :] = tile
         msg_ref[2 * h + 1, 16:, :] = tile
@@ -74,14 +73,18 @@
     lane = lax.broadcasted_iota(jnp.int32, (HEAD_DIM, CHUNK), 1)
     inside = [lane >= k for k in range(4)]
 
+    all_taps = taps_ref[...] * 0.5
+    all_bias = jnp.transpose(jnp.broadcast_to(bias_ref[...] * 0.5, (8, ROWS)))
+
     def one_head(head):
-        rows = pl.ds(pl.multiple_of(head * HEAD_DIM, HEAD_DIM), HEAD_DIM)
-        taps = jnp.broadcast_to(taps_ref[head, :1, :], (HEAD_DIM, 4 * HEAD_DIM))
+        rows = slice(head * HEAD_DIM, (head + 1) * HEAD_DIM)
+        taps = jnp.concatenate([all_taps[k : k + 1, rows] for k in range(4)], axis=1)
+        taps = jnp.broadcast_to(taps, (HEAD_DIM, 4 * HEAD_DIM))
         taps = jnp.where(diagonal, taps, 0.0)
         taps_hi = taps.astype(BF16)
         taps_low = (taps - taps_hi.astype(F32)).astype(BF16)
         left = jnp.concatenate([taps_hi, taps_low], axis=0)
-        bias = jnp.broadcast_to(bias_ref[rows, :1], (HEAD_DIM, 2 * CHUNK))
+        bias = jnp.broadcast_to(all_bias[rows, :1], (HEAD_DIM, 2 * CHUNK))
         last = halo_ref[rows, :]
         prior = [None] + [pltpu.roll(last, k, 1) for k in (1, 2, 3)]
         for t in range(chunks // 2):
@@ -101,12 +104,8 @@
             to_end = jnp.concatenate([to_end] * 8, axis=0)
             xd_scr[rows, at] = (value * to_end).astype(BF16)
 
-    def body(pair, carry):
-        for k in range(UNROLL):
-            one_head(pair * UNROLL + k)
-        return carry
-
-    lax.fori_loop(0, GROUP // UNROLL, body, 0)
+    for head in range(GROUP):
+        one_head(head)
     states = dot_nt(xd_scr[...], keys).astype(BF16)
     for k in range(2 * GROUP):
         msg_ref[k, :16, :] = jnp.concatenate(
@@ -119,7 +118,7 @@
     for d in range(got_ref.shape[0]):
         out_ref[d] = entering.astype(BF16)
         parts = got_ref[d, 16:, :].astype(F32)
-        decay = parts[:8] + parts[8:]
+        decay = parts + pltpu.roll(parts, 4, 0)
         decay = jnp.concatenate([decay, decay], axis=0)
         entering = decay * entering + got_ref[d, :16, :].astype(F32)
 
@@ -199,16 +198,29 @@
     lax.fori_loop(0, chunks // CHUNKS_PER_STEP, body, 0)
 
 
-def carried_kernel(chunks, y_ref, maps_ref, lead_ref, enter_ref, out_ref):
+def carried_group(chunks, y_ref, maps_ref, lead_ref, enter_ref, out_ref):
     entering = head_states(enter_ref)
     for c in range(chunks // 2):
         at = slice(c * 256, (c + 1) * 256)
-        queries = maps_ref[STATE:, at]
-        carried = jnp.dot(entering, queries, preferred_element_type=F32)
+        carried = jnp.dot(entering, maps_ref[STATE:, at], preferred_element_type=F32)
         for h in range(GROUP):
             rows = slice(h * HEAD_DIM, (h + 1) * HEAD_DIM)
             add = carried[rows] * lead_ref[h : h + 1, at]
             out_ref[rows, at] = (y_ref[rows, at].astype(F32) + add).astype(BF16)
+
+
+def last_kernel(chunks, late, x_ref, maps_ref, step_ref, sums_ref, skip_ref, enter_ref, y_ref, lead_ref,
+                out_ref, state_scr):
+    g = pl.program_id(0)
+    is_late = (lax.rem(g, 2) == 0) & (g < 2 * late)
+
+    @pl.when(is_late)
+    def _():
+        local_kernel(chunks, True, x_ref, maps_ref, step_ref, sums_ref, skip_ref, enter_ref, out_ref, state_scr)
+
+    @pl.when(jnp.logical_not(is_late))
+    def _():
+        carried_group(chunks, y_ref, maps_ref, lead_ref, enter_ref, out_ref)
 
 
 def local(raw_inputs, state_maps, step_size, log_decay, conv_weight, conv_bias, skip_gain, axis):
@@ -222,10 +234,6 @@
         raw_inputs[:, tokens - 3 :], axis, [(i, i + 1) for i in range(count - 1)]
     )
     halo = jnp.pad(tail, ((0, 0), (CHUNK - 3, 0)))
-
-    taps = 0.5 * jnp.transpose(conv_weight.reshape(4, heads, HEAD_DIM), (1, 0, 2))
-    taps = taps.reshape(heads, 1, 4 * HEAD_DIM)
-    bias = jnp.broadcast_to(0.5 * conv_bias[:, None], (channels, 128))
 
     block = lambda g: (g, 0)
     whole = lambda g: (0, 0)
@@ -246,15 +254,15 @@
             maps,
             rows8,
             rows8,
-            pl.BlockSpec((GROUP, 1, 4 * HEAD_DIM), lambda g: (g, 0, 0)),
-            pl.BlockSpec((ROWS, 128), block),
+            pl.BlockSpec((4, ROWS), lambda g: (0, g)),
+            pl.BlockSpec((1, ROWS), lambda g: (0, g)),
         ],
-        out_specs=[big, rows8, rows8, pl.BlockSpec((2 * GROUP, 32, 128), lambda g: (g, 0, 0))],
+        out_specs=[big, rows8, rows8, pl.BlockSpec((2 * GROUP, 24, 128), lambda g: (g, 0, 0))],
         out_shape=[
             jax.ShapeDtypeStruct((channels, tokens), BF16),
             jax.ShapeDtypeStruct((heads, tokens), F32),
             jax.ShapeDtypeStruct((heads, tokens), F32),
-            jax.ShapeDtypeStruct((count, 32, 128), BF16),
+            jax.ShapeDtypeStruct((count, 24, 128), BF16),
         ],
         scratch_shapes=[
             pltpu.VMEM((GROUP, 8, tokens), F32),
@@ -263,7 +271,7 @@
         compiler_params=params,
         cost_estimate=cost(20),
         name="values",
-    )(raw_inputs, halo, state_maps, step_size, log_decay, taps, bias)
+    )(raw_inputs, halo, state_maps, step_size, log_decay, conv_weight, conv_bias.reshape(1, channels))
 
     got = lax.all_to_all(message, axis, 0, 0, tiled=True)
 
@@ -314,24 +322,40 @@
     back = lax.all_to_all(entering, axis, 0, 0, tiled=True)
 
     partial = local_part(early, middle - early, partial)
-    partial = local_part(middle, groups - middle, partial, back)
-
+    late = groups - middle
+
+    def late_group(g):
+        return middle + jnp.minimum((g + 1) // 2, late - 1)
+
+    def early_group(g):
+        return jnp.where(g >= 2 * late, g - late, jnp.maximum(g - 1, 0) // 2)
+
+    def own_group(g):
+        return jnp.where((g % 2 == 0) & (g < 2 * late), late_group(g), early_group(g))
+
+    at_late = lambda g: (late_group(g), 0)
+    at_early = lambda g: (early_group(g), 0)
     return pl.pallas_call(
-        functools.partial(carried_kernel, chunks),
-        grid=(middle,),
+        functools.partial(last_kernel, chunks, late),
+        grid=(groups,),
         in_specs=[
-            big,
+            pl.BlockSpec((ROWS, tokens), at_late),
             maps,
-            rows8,
-            pl.BlockSpec((2 * GROUP, 16, 128), lambda g: (g, 0, 0)),
+            pl.BlockSpec((GROUP, tokens), at_late),
+            pl.BlockSpec((GROUP, tokens), at_late),
+            pl.BlockSpec((GROUP, CHUNK), at_late),
+            pl.BlockSpec((2 * GROUP, 16, 128), lambda g: (own_group(g), 0, 0)),
+            pl.BlockSpec((ROWS, tokens), at_early),
+            pl.BlockSpec((GROUP, tokens), at_early),
         ],
-        out_specs=big,
+        out_specs=pl.BlockSpec((ROWS, tokens), lambda g: (own_group(g), 0)),
         out_shape=jax.ShapeDtypeStruct((channels, tokens), BF16),
-        input_output_aliases={0: 0},
+        scratch_shapes=[pltpu.VMEM((ROWS, STATE), F32)],
+        input_output_aliases={6: 0},
         compiler_params=params,
-        cost_estimate=cost(8),
-        name="carried",
-    )(partial, state_maps, lead, back)
+        cost_estimate=cost(20),
+        name="last",
+    )(values, state_maps, step_size, sums, skip, back, partial, lead)
 
 
 def solution(mesh):

time: 113 us -> 108 us (0.956)
  waiting for transfers between devices: 8.22 us -> 5.26 us
  starting transfers between devices: 19.2 us -> 21.1 us
  other arithmetic: 1.56 us -> 0 us
  local copies, waits for them, and re-layouts: 8.78 us -> 7.37 us
    pallas_call x3 -> x2, Pallas kernels: 40.2 us -> 23.9 us  [local_part(): pl.pallas_call(functools.partial(local_kernel, chunks, enter is not None)...]
    pallas_call x1, Pallas kernels: 7.81 us -> 22.6 us  [local(): pl.pallas_call(functools.partial(last_kernel, chunks, late), grid=(groups...]
    all_to_all x1, waiting for transfers between devices: 6.8 us -> 3.98 us  [local(): got = lax.all_to_all(message, axis, 0, 0, tiled=True)]
    broadcast_in_dim x1 -> x0, local copies, waits for them, and re-layouts: 1.77 us -> none  [local(): bias = jnp.broadcast_to(0.5 * conv_bias[:, None], (channels, 128))]
    mul x2 -> x0, other arithmetic: 1.56 us -> none  [the longest x1 0.83 us: local(): 0.5 * jnp.transpose(conv_weight.reshape(4, heads, HEAD_DIM), (1, 0, 2))]
    all_to_all x1, starting transfers between devices: 4.64 us -> 5.78 us  [local(): back = lax.all_to_all(entering, axis, 0, 0, tiled=True)]
  transfers between devices with their start and end apart: 3 -> 3, of which waited for: 2 -> 2; matrix products, arithmetic and copies ran while one was open for 3% -> 2% of each run, Pallas kernels for 21% -> 22%
where the time goes in v3:
time: 108 us
  Pallas kernels  74 us (69%)
  starting transfers between devices  21.1 us (20%)
  local copies, waits for them, and re-layouts  7.37 us (7%)
  waiting for transfers between devices  5.26 us (5%)
    pallas_call x1, Pallas kernels, local(): pl.pallas_call(functools.partial(values_kernel, chunks), grid=(groups,),...  25.2 us
    pallas_call x2, Pallas kernels, local_part(): pl.pallas_call(functools.partial(local_kernel, chunks, enter is not None)...  23.9 us
    pallas_call x1, Pallas kernels, local(): pl.pallas_call(functools.partial(last_kernel, chunks, late), grid=(groups...  22.6 us
    all_to_all x1, starting transfers between devices, local(): got = lax.all_to_all(message, axis, 0, 0, tiled=True)  10.4 us
    all_to_all x1, starting transfers between devices, local(): back = lax.all_to_all(entering, axis, 0, 0, tiled=True)  5.78 us
    ppermute x1, starting transfers between devices, local(): lax.ppermute(raw_inputs[:, tokens - 3:], axis, [(i, i + 1) for i in range...  4.92 us
    all_to_all x1, waiting for transfers between devices, local(): got = lax.all_to_all(message, axis, 0, 0, tiled=True)  3.98 us
    pallas_call x1, Pallas kernels, local(): pl.pallas_call(scan_kernel, in_specs=[pl.BlockSpec(memory_space=pltpu.VME...  2.2 us
  transfers between devices with their start and end apart: 3, of which 2 were waited for; matrix products, arithmetic and copies ran while one was open for 2% of the time, Pallas kernels for 22%

profile of v3, /device:TPU:1, one launch (start us, length us, event | category | flops | bytes accessed | tf_op | source)
XLA Modules:
  0.0 107.8 jit_solution(17151518622700910842)
XLA Ops:
  0.0 1.5 %slice.3 = bf16[3584,3]{1,0:T(8,128)(2,1)S(1)} slice(bf16[3584,1792]{1,0:T(8,128)(2,1)} %raw_ref.1), slice={[0:3584], [1789:1792]} | slice | bytes 43008 | tf_op jit(solution)/shard_map/slice | solution.py:234
  1.5 0.3 copy.12
  1.8 4.9 %collective-permute-start = (bf16[3584,3]{0,1:T(4,128)(2,1)S(1)}, bf16[3584,3]{0,1:T(4,128)(2,1)S(1)}, u32[]{:S(2)}, u32[]{:S(2)}) collective-permute-start(bf16[3584,3]{0,1:T(4,128)(2,1)S(1)} %copy.12), channel_id=1, source_target_pairs={{0,1},{1,2},{2,3},{3,4},{4,5},{5,6},{6,7},{7,8},{8,9},{9,10},{10,1... | collective-permute-start | bytes 64520 | tf_op jit(solution)/shard_map/ppermute | solution.py:233
  6.8 1.3 %reshape.4.bias_ref = f32[1,3584]{1,0:T(1,128)} reshape(f32[3584]{0:T(1024)} %param.12) | data formatting | bytes 28672 | tf_op jit(solution)/shard_map/reshape | solution.py:274
  8.1 0.0 collective-permute-done
  8.1 0.5 copy.11
  8.6 1.3 %pad.4.halo_ref = bf16[3584,128]{1,0:T(8,128)(2,1)} pad(bf16[3584,3]{1,0:T(8,128)(2,1)S(1)} %copy.11, bf16[]{:T(256)} %constant.2.clone.1), padding=0_0x125_0 | pad | bytes 939010 | tf_op jit(solution)/shard_map/jit(_pad)/pad | solution.py:236
  9.8 0.0 copy-start.2
  9.8 25.2 %values.1 = (bf16[3584,1792]{1,0:T(8,128)(2,1)}, f32[56,1792]{1,0:T(8,128)}, f32[56,1792]{1,0:T(8,128)}, bf16[128,24,128]{2,1,0:T(8,128)(2,1)}) custom-call(bf16[3584,1792]{1,0:T(8,128)(2,1)} %raw_ref.1, bf16[3584,128]{1,0:T(8,128)(2,1)} %pad.4.halo_ref, bf16[128,1792]{1,0:T(8,128)(2,1)} %maps_ref.3, f32[56,1792]{1,0:T(8,128)} %step_ref.3, ...), custom_call_target="tpu_custom_call" | custom-call | flops 10000000000 | bytes 20000000 | tf_op jit(solution)/shard_map/values/pallas_call | solution.py:248
  35.1 10.4 %all-to-all-start = ((bf16[128,24,128]{2,1,0:T(8,128)(2,1)}), bf16[128,24,128]{2,1,0:T(8,128)(2,1)S(1)}, u32[]{:S(2)}, u32[]{:S(2)}) async-start(bf16[128,24,128]{2,1,0:T(8,128)(2,1)} %get-tuple-element.11), calls=%async_computation | async-start | bytes 1572864 | tf_op jit(solution)/shard_map/all_to_all | solution.py:276
  45.5 0.0 copy-done.2
  45.5 0.7 broadcast_in_dim.2.refs_4_.skip_ref
  46.2 11.7 %inside.2.refs_5_ = bf16[3584,1792]{1,0:T(8,128)(2,1)} custom-call(bf16[3584,1792]{1,0:T(8,128)(2,1)} %get-tuple-element.9.refs_0_.x_ref, bf16[128,1792]{1,0:T(8,128)(2,1)} %maps_ref.3, f32[56,1792]{1,0:T(8,128)} %step_ref.3, f32[56,1792]{1,0:T(8,128)} %get-tuple-element.10.refs_3_.sums_ref, f32[56,128]{1,0:T(8,128)} %broadcast_in_dim.2.refs_4_.skip_ref), custom_call_target="tpu_custom_call" | custom-call | flops 8000000000 | bytes 16000000 | tf_op jit(solution)/shard_map/inside/pallas_call | solution.py:298
  57.9 4.0 %all-to-all-done.got_ref = bf16[128,24,128]{2,1,0:T(8,128)(2,1)S(1)} async-done(((bf16[128,24,128]{2,1,0:T(8,128)(2,1)}), bf16[128,24,128]{2,1,0:T(8,128)(2,1)S(1)}, u32[]{:S(2)}, u32[]{:S(2)}) %all-to-all-start) | async-done | bytes 786464 | tf_op jit(solution)/shard_map/all_to_all | solution.py:276
  61.9 0.0 copy-start.1
  61.9 0.9 copy-done.1
  62.8 2.2 %scan.1 = bf16[128,16,128]{2,1,0:T(8,128)(2,1)} custom-call(bf16[128,24,128]{2,1,0:T(8,128)(2,1)} %copy-done.1), custom_call_target="tpu_custom_call" | custom-call | flops 1500000000 | bytes 3000000 | tf_op jit(solution)/shard_map/scan/pallas_call | solution.py:314
  65.0 5.8 %all-to-all-start.1 = ((bf16[128,16,128]{2,1,0:T(8,128)(2,1)}), bf16[128,16,128]{2,1,0:T(8,128)(2,1)S(1)}, u32[]{:S(2)}, u32[]{:S(2)}) async-start(bf16[128,16,128]{2,1,0:T(8,128)(2,1)} %scan.1), calls=%async_computation.1 | async-start | bytes 1048576 | tf_op jit(solution)/shard_map/all_to_all | solution.py:322
  70.8 12.3 %inside.3.y_ref = bf16[3584,1792]{1,0:T(8,128)(2,1)} custom-call(bf16[3584,1792]{1,0:T(8,128)(2,1)} %get-tuple-element.9.refs_0_.x_ref, bf16[128,1792]{1,0:T(8,128)(2,1)} %maps_ref.3, f32[56,1792]{1,0:T(8,128)} %step_ref.3, f32[56,1792]{1,0:T(8,128)} %get-tuple-element.10.refs_3_.sums_ref, ...), custom_call_target="tpu_custom_call", output_to_operand_aliasing={{}: (5, {})} | custom-call | flops 8000000000 | bytes 16000000 | tf_op jit(solution)/shard_map/inside/pallas_call | solution.py:298
  83.1 1.3 %all-to-all-done.1.enter_ref = bf16[128,16,128]{2,1,0:T(8,128)(2,1)S(1)} async-done(((bf16[128,16,128]{2,1,0:T(8,128)(2,1)}), bf16[128,16,128]{2,1,0:T(8,128)(2,1)S(1)}, u32[]{:S(2)}, u32[]{:S(2)}) %all-to-all-start.1) | async-done | bytes 524320 | tf_op jit(solution)/shard_map/all_to_all | solution.py:322
  84.4 0.0 copy-start
  84.4 0.8 copy-done
  85.2 22.6 %last.1 = bf16[3584,1792]{1,0:T(8,128)(2,1)} custom-call(bf16[3584,1792]{1,0:T(8,128)(2,1)} %get-tuple-element.9.refs_0_.x_ref, bf16[128,1792]{1,0:T(8,128)(2,1)} %maps_ref.3, f32[56,1792]{1,0:T(8,128)} %step_ref.3, f32[56,1792]{1,0:T(8,128)} %get-tuple-element.10.refs_3_.sums_ref, ...), custom_call_target="tpu_custom_call", output_to_operand_aliasing={{}: (6, {})} | custom-call | flops 10000000000 | bytes 20000000 | tf_op jit(solution)/shard_map/last/pallas_call | solution.py:338
Async XLA Ops:
  1.8 6.3 %collective-permute-start = (bf16[3584,3]{0,1:T(4,128)(2,1)S(1)}, bf16[3584,3]{0,1:T(4,128)(2,1)S(1)}, u32[]{:S(2)}, u32[]{:S(2)}) collective-permute-start(bf16[3584,3]{0,1:T(4,128)(2,1)S(1)} %copy.12), channel_id=1, source_target_pairs={{0,1},{1,2},{2,3},{3,4},{4,5},{5,6},{6,7},{7,8},{8,9},{9,10},{10,1... | collective-permute-start | bytes 64520 | tf_op jit(solution)/shard_map/ppermute | solution.py:233
  9.8 35.7 %copy-start.2 = (f32[56]{0:T(128)S(1)}, f32[56]{0:T(128)}, u32[]{:S(2)}) copy-start(f32[56]{0:T(128)} %param.13) | copy-start | bytes 676
  35.1 26.8 %all-to-all-start = ((bf16[128,24,128]{2,1,0:T(8,128)(2,1)}), bf16[128,24,128]{2,1,0:T(8,128)(2,1)S(1)}, u32[]{:S(2)}, u32[]{:S(2)}) async-start(bf16[128,24,128]{2,1,0:T(8,128)(2,1)} %get-tuple-element.11), calls=%async_computation | async-start | bytes 1572864 | tf_op jit(solution)/shard_map/all_to_all | solution.py:276
  61.9 0.9 copy-start.1
  65.0 19.3 %all-to-all-start.1 = ((bf16[128,16,128]{2,1,0:T(8,128)(2,1)}), bf16[128,16,128]{2,1,0:T(8,128)(2,1)S(1)}, u32[]{:S(2)}, u32[]{:S(2)}) async-start(bf16[128,16,128]{2,1,0:T(8,128)(2,1)} %scan.1), calls=%async_computation.1 | async-start | bytes 1048576 | tf_op jit(solution)/shard_map/all_to_all | solution.py:322
  84.4 0.8 copy-start
